TPU v7x, 32 devices: a whole 2x2x4 slice. The times are simulated.
32 devices in a mesh: groups: 2 (over y), section: 4 (over z), seq: 4 (over x, core).
Axes of the slice: x: 2, y: 2, z: 4, core: 2. Of those that a mesh axis runs over, the one named last changes fastest.
Arguments:
- tokens: bfloat16 [8, 256, 1440], P('groups', 'seq'), parts along dimension 0, may hold values from -6 to 6
- block_order: int32 [8], P('groups'), parts along dimension 0, may hold values from 0 to 3, each once
- prompt_lengths: int32 [8], P('groups'), parts along dimension 0, may hold values from 1 to 256, 576 in all
- norm_gain: float32 [4, 1440], P('section'), may hold values from 0.1 to 1.9
- w_query: bfloat16 [4, 1440, 2048], P('section', None, 'seq'), may hold values from -4 to 4
- w_key_value: bfloat16 [4, 1440, 512], P('section'), may hold values from -4 to 4
- w_out: bfloat16 [4, 2048, 1440], P('section', 'seq'), may hold values from -0.125 to 0.125
- sink_logits: float32 [4, 32], P('section'), may hold values from 0 to 4
Outputs:
- hidden_states: bfloat16 [4, 8, 256, 1440], P('section', 'groups', 'seq'), parts along dimension 1
- layer_cache: bfloat16 [4, 8, 256, 512], P('section', 'groups', 'seq'), parts along dimension 1
There are 2 independent parts, one for each index of `groups`. A program takes and returns all parts, laid end to end along the dimension named above; an argument that names none is the same for every part. Nothing has to cross between parts.
Inputs may be any that keep to these rules, and one draw needn't show every extreme that they name: `block_order`: each of 0 to 3 exactly once. `prompt_lengths`: the longest prompt is full.
All inputs are finite; a program needn't handle non-finite values.
Results may differ from a plain program's by a relative error of at most 0.024.
Values may be sent and summed in bfloat16 or wider, within the bound.
No kernel may reach another device: no remote copies, remote signals or barrier semaphores. Data moves between devices by JAX's collectives and lax.ppermute only.
A program may use at most 128 MiB of HBM per device.

v0:
```python
import math
import jax
import jax.numpy as jnp
from jax import lax
from jax.sharding import PartitionSpec as P

HEAD_DIM = 64
WIN = 128
THETA = 150000.0
EPSILON = 1e-05


def from_behind(block, axis, distance):
    devices = range(lax.axis_size(axis))
    route = [(i - distance, i) for i in devices if i - distance in devices]
    return lax.ppermute(block, axis, route)


def rotary(positions, head_size):
    half = head_size // 2
    freq = jnp.exp(jnp.arange(half, dtype=jnp.float32) * (-2.0 * math.log(THETA) / head_size))
    angles = positions.astype(jnp.float32)[:, None] * freq[None, :]
    return (jnp.cos(angles)[:, None, :], jnp.sin(angles)[:, None, :])


def rotate(values, cosine, sine):
    half = values.shape[-1] // 2
    first = values[..., :half]
    second = values[..., half:]
    return jnp.concatenate([first * cosine - second * sine, second * cosine + first * sine], -1)


def per_device(
    tokens, block_order, prompt_lengths, norm_gain, w_query, w_key_value, w_out, sink_logits
):
    section_index = lax.axis_index("section")
    sections = lax.axis_size("section")
    seq_index = lax.axis_index("seq")
    micro, rows, width = tokens.shape
    full_query, full_out = (
        lax.all_gather(w_query, "seq", axis=2, tiled=True),
        lax.all_gather(w_out, "seq", axis=1, tiled=True),
    )
    query_weight = full_query[0]
    out_weight = full_out[0]
    pair_weight = w_key_value[0]
    gain = norm_gain[0]
    heads_width = query_weight.shape[1]
    head_count = heads_width // HEAD_DIM
    kv_width = pair_weight.shape[1] // 2
    kv_heads = kv_width // HEAD_DIM
    group = head_count // kv_heads
    sink = sink_logits[0].reshape(kv_heads, group)[:, :, None]
    keep = min(WIN, rows)
    depth = WIN // keep
    start = seq_index * rows
    positions = start + jnp.arange(rows, dtype=jnp.int32)
    cosine, sine = rotary(positions, HEAD_DIM)
    key_positions = start - WIN + jnp.arange(WIN + rows, dtype=jnp.int32)

    def project(hidden):
        widened = hidden.astype(jnp.float32)
        scale = lax.rsqrt(jnp.mean(widened * widened, -1, keepdims=True) + EPSILON)
        normed = (widened * scale * gain).astype(jnp.bfloat16)
        queries = jnp.dot(normed, query_weight, preferred_element_type=jnp.float32).reshape(
            rows, head_count, HEAD_DIM
        )
        queries = rotate(queries, cosine, sine).astype(jnp.bfloat16).reshape(rows, heads_width)
        projected = jnp.dot(normed, pair_weight, preferred_element_type=jnp.float32)
        rotated = rotate(
            projected[:, :kv_width].reshape(rows, kv_heads, HEAD_DIM), cosine, sine
        ).reshape(rows, kv_width)
        cache = jnp.concatenate([rotated, projected[:, kv_width:]], 1).astype(jnp.bfloat16)
        return (queries, cache)

    def project_spare(hidden):
        return (
            jnp.zeros((rows, heads_width), jnp.bfloat16),
            jnp.zeros((rows, 2 * kv_width), jnp.bfloat16),
        )

    def window_of(cache):
        pieces = [from_behind(cache, "seq", offset) for offset in range(depth, 0, -1)]
        return jnp.concatenate(pieces, 0)

    def attend(operands):
        hidden, queries, cache, window, length = operands
        joined = jnp.concatenate([window, cache], 0)
        key_heads = joined[:, :kv_width].reshape(WIN + rows, kv_heads, HEAD_DIM)
        value_heads = joined[:, kv_width:].reshape(WIN + rows, kv_heads, HEAD_DIM)
        grouped = queries.reshape(rows, kv_heads, group, HEAD_DIM)
        scores = (
            jnp.einsum("qkgd,skd->kgqs", grouped, key_heads, preferred_element_type=jnp.float32)
            * 0.125
        )
        query_col = positions[:, None]
        key_row = key_positions[None, :]
        allowed = (key_row <= query_col) & (query_col - key_row < WIN) & (key_row >= 0)
        allowed = allowed & ((key_row < length) | (key_row == query_col))
        masked = jnp.where(allowed, scores, jnp.float32(-1e30))
        top = jnp.maximum(jnp.max(masked, -1), sink)
        expo = jnp.where(allowed, jnp.exp(scores - top[..., None]), jnp.float32(0.0))
        total = jnp.sum(expo, -1) + jnp.exp(sink - top)
        weights = (expo / total[..., None]).astype(jnp.bfloat16)
        context = jnp.einsum(
            "kgqs,skd->qkgd", weights, value_heads, preferred_element_type=jnp.float32
        )
        context = context.reshape(rows, heads_width).astype(jnp.bfloat16)
        output = jnp.dot(context, out_weight, preferred_element_type=jnp.float32)
        return (hidden.astype(jnp.float32) + output).astype(jnp.bfloat16)

    def pass_through(operands):
        return operands[0]

    def turn(counter, carry):
        arriving, hidden_buffer, cache_buffer = carry
        slot = counter - section_index
        active = (slot >= 0) & (slot < micro)
        slot_safe = jnp.clip(slot, 0, micro - 1)
        block = block_order[slot_safe]
        length = prompt_lengths[block]
        entering = lax.dynamic_index_in_dim(tokens, block, 0, keepdims=False)
        hidden = jnp.where(section_index == 0, entering, arriving)
        queries, cache = lax.cond(active, project, project_spare, hidden)
        window = window_of(cache)
        updated = lax.cond(active, attend, pass_through, (hidden, queries, cache, window, length))
        previous_hidden = lax.dynamic_index_in_dim(hidden_buffer, slot_safe, 0, keepdims=False)
        previous_cache = lax.dynamic_index_in_dim(cache_buffer, slot_safe, 0, keepdims=False)
        hidden_buffer = lax.dynamic_update_index_in_dim(
            hidden_buffer, jnp.where(active, updated, previous_hidden), slot_safe, 0
        )
        cache_buffer = lax.dynamic_update_index_in_dim(
            cache_buffer, jnp.where(active, cache, previous_cache), slot_safe, 0
        )
        passed = from_behind(updated, "section", 1)
        return (passed, hidden_buffer, cache_buffer)

    initial = (
        jnp.zeros((rows, width), jnp.bfloat16),
        jnp.zeros((micro, rows, width), jnp.bfloat16),
        jnp.zeros((micro, rows, 2 * kv_width), jnp.bfloat16),
    )
    final = lax.fori_loop(0, micro + sections - 1, turn, initial)
    return (final[1][None], final[2][None])


def solution(mesh):
    in_specs = (
        P("groups", "seq", None),
        P("groups"),
        P("groups"),
        P("section", None),
        P("section", None, "seq"),
        P("section", None, None),
        P("section", "seq", None),
        P("section", None),
    )
    out_specs = (P("section", "groups", "seq", None), P("section", "groups", "seq", None))
    return jax.shard_map(
        per_device, mesh=mesh, in_specs=in_specs, out_specs=out_specs, check_vma=False
    )
```

profile of v0, /device:TPU:28, one launch (start us, length us, event | category | flops | bytes accessed | tf_op | source)
XLA Modules:
  0.0 363.9 jit_solution(2830805438816558788)
XLA Ops:
  8.5 1.6 copy.14
  11.5 43.2 %all-gather.3.cloned.1.call-done = bf16[1,1440,2048]{2,1,0:T(8,128)(2,1)} async-done(((bf16[1,1440,512]{2,1,0:T(8,128)(2,1)}), bf16[1,1440,2048]{2,1,0:T(8,128)(2,1)}) %all-gather.3.cloned.1.call-update) | async-done | bytes 5898256 | tf_op jit(solution)/shard_map/all_gather | solution.py:41
  54.6 47.9 %all-gather.5.cloned.1.call-done = bf16[1,2048,1440]{2,1,0:T(8,128)(2,1)} async-done(((bf16[1,512,1440]{2,1,0:T(8,128)(2,1)}), bf16[1,2048,1440]{2,1,0:T(8,128)(2,1)}) %all-gather.5.cloned.1.call-update) | async-done | bytes 5898256 | tf_op jit(solution)/shard_map/all_gather | solution.py:42
  104.3 252.8 %while.20 = (s32[]{:T(128)}, bf16[64,1440]{1,0:T(8,128)(2,1)S(1)}, bf16[4,64,1440]{2,1,0:T(8,128)(2,1)}, bf16[4,64,512]{2,1,0:T(8,128)(2,1)}, s32[]{:T(128)}, /*...) while((s32[]{:T(128)}, bf16[64,1440]{1,0:T(8,128)(2,1)S(1)}, ...), condition=%wide.region_8.9_spmd.clone.clone, body=%wide.region_0.8_spmd.clone.clone.sunk | while | flops 958372544 | bytes 47880768 | solution.py:143
  107.8 1.4 conditional.8
  109.1 2.5 collective-permute-start
  111.6 1.9 collective-permute-start.1
  116.0 1.3 collective-permute-start.2
  118.0 7.3 %collective-permute-done.2 = bf16[64,1440]{1,0:T(8,128)(2,1)S(1)} collective-permute-done((bf16[64,1440]{1,0:T(8,128)(2,1)S(1)}, bf16[64,1440]{1,0:T(8,128)(2,1)S(1)}, u32[]{:S(2)}, u32[]{:S(2)}) %collective-permute-start.2) | collective-permute-done | bytes 184352 | tf_op jit(solution)/shard_map/while/body/eval_jaxpr/ppermute | solution.py:16
  128.8 1.4 conditional.8
  130.1 3.0 collective-permute-start
  133.2 1.3 collective-permute-start.1
  137.0 1.3 collective-permute-start.2
  139.0 7.2 %collective-permute-done.2 = bf16[64,1440]{1,0:T(8,128)(2,1)S(1)} collective-permute-done((bf16[64,1440]{1,0:T(8,128)(2,1)S(1)}, bf16[64,1440]{1,0:T(8,128)(2,1)S(1)}, u32[]{:S(2)}, u32[]{:S(2)}) %collective-permute-start.2) | collective-permute-done | bytes 184352 | tf_op jit(solution)/shard_map/while/body/eval_jaxpr/ppermute | solution.py:16
  149.6 1.4 conditional.8
  151.0 3.0 collective-permute-start
  154.0 1.3 collective-permute-start.1
  157.8 1.3 collective-permute-start.2
  159.8 50.5 %collective-permute-done.2 = bf16[64,1440]{1,0:T(8,128)(2,1)S(1)} collective-permute-done((bf16[64,1440]{1,0:T(8,128)(2,1)S(1)}, bf16[64,1440]{1,0:T(8,128)(2,1)S(1)}, u32[]{:S(2)}, u32[]{:S(2)}) %collective-permute-start.2) | collective-permute-done | bytes 184352 | tf_op jit(solution)/shard_map/while/body/eval_jaxpr/ppermute | solution.py:16
  213.8 9.2 %conditional.8 = (bf16[64,2048]{1,0:T(8,128)(2,1)S(1)}, bf16[64,512]{1,0:T(8,128)(2,1)}, bf16[64,512]{0,1:T(8,128)(2,1)}) conditional(s32[]{:T(128)} %convert_element_type.69, () %tuple.79, (bf16[64,1440]{1,0:T(8,128)(2,1)S(1)}, f32[1,1440]{1,0:T(1,128)S(1)}, bf16[1440,2048]{1,0:T(8,128)(2,1)}, f32[64,1,32]{2,0,1:T(8,128)S(1)}, ...), branch_computations={%region_1.1_spmd, %region_2.3_spmd} | conditional | flops 474183744 | bytes 12373788 | solution.py:124
  214.0 3.9 %fusion.26 = f32[64,2048]{1,0:T(8,128)S(1)} fusion(bf16[1440,2048]{1,0:T(8,128)(2,1)} %get-tuple-element.374, bf16[64,1440]{1,0:T(8,128)(2,1)S(1)} %get-tuple-element.372, f32[1440]{0:T(1024)S(1)} %reduce, f32[64]{0:T(128)S(1)} %add_rsqrt_fusion), kind=kOutput, calls=%fused_computation.44 | convolution fusion | flops 377856000 | bytes 6612864 | tf_op jit(solution)/shard_map/while/body/eval_jaxpr/cond/branch_1_fun/dot_general | solution.py:65
  221.4 1.6 copy.18
  223.0 2.3 collective-permute-start
  225.4 1.3 collective-permute-start.1
  228.5 1.5 bitcast_dynamic-update-slice_fusion.5
  230.0 8.0 %conditional.9 = (bf16[64,1440]{1,0:T(8,128)(2,1)S(1)}) conditional(s32[]{:T(128)} %convert_element_type.69, bf16[64,1440]{1,0:T(8,128)(2,1)S(1)} %bitcast_select_fusion.5, (bf16[64,1440]{1,0:T(8,128)(2,1)S(1)}, bf16[64,512]{0,1:T(8,128)(2,1)S(1)}, bf16[64,512]{0,1:T(8,128)(2,1)S(1)}, bf16[64,512]{1,0:T(8,128)(2,1)}, s32[]{:T(128)}, ...), branch_computations={%region_4.4_spmd, %region_5.7_spmd} | conditional | flops 483969664 | bytes 32420688 | solution.py:126
  234.5 1.1 convolution_convert_fusion
  236.7 1.2 fusion.8
  238.0 1.3 collective-permute-start.2
  240.0 7.1 %collective-permute-done.2 = bf16[64,1440]{1,0:T(8,128)(2,1)S(1)} collective-permute-done((bf16[64,1440]{1,0:T(8,128)(2,1)S(1)}, bf16[64,1440]{1,0:T(8,128)(2,1)S(1)}, u32[]{:S(2)}, u32[]{:S(2)}) %collective-permute-start.2) | collective-permute-done | bytes 184352 | tf_op jit(solution)/shard_map/while/body/eval_jaxpr/ppermute | solution.py:16
  250.6 9.2 %conditional.8 = (bf16[64,2048]{1,0:T(8,128)(2,1)S(1)}, bf16[64,512]{1,0:T(8,128)(2,1)}, bf16[64,512]{0,1:T(8,128)(2,1)}) conditional(s32[]{:T(128)} %convert_element_type.69, () %tuple.79, (bf16[64,1440]{1,0:T(8,128)(2,1)S(1)}, f32[1,1440]{1,0:T(1,128)S(1)}, bf16[1440,2048]{1,0:T(8,128)(2,1)}, f32[64,1,32]{2,0,1:T(8,128)S(1)}, ...), branch_computations={%region_1.1_spmd, %region_2.3_spmd} | conditional | flops 474183744 | bytes 12373788 | solution.py:124
  250.8 3.9 %fusion.26 = f32[64,2048]{1,0:T(8,128)S(1)} fusion(bf16[1440,2048]{1,0:T(8,128)(2,1)} %get-tuple-element.374, bf16[64,1440]{1,0:T(8,128)(2,1)S(1)} %get-tuple-element.372, f32[1440]{0:T(1024)S(1)} %reduce, f32[64]{0:T(128)S(1)} %add_rsqrt_fusion), kind=kOutput, calls=%fused_computation.44 | convolution fusion | flops 377856000 | bytes 6612864 | tf_op jit(solution)/shard_map/while/body/eval_jaxpr/cond/branch_1_fun/dot_general | solution.py:65
  258.2 1.6 copy.18
  259.8 2.3 collective-permute-start
  262.1 1.3 collective-permute-start.1
  265.2 1.5 bitcast_dynamic-update-slice_fusion.5
  266.7 8.0 %conditional.9 = (bf16[64,1440]{1,0:T(8,128)(2,1)S(1)}) conditional(s32[]{:T(128)} %convert_element_type.69, bf16[64,1440]{1,0:T(8,128)(2,1)S(1)} %bitcast_select_fusion.5, (bf16[64,1440]{1,0:T(8,128)(2,1)S(1)}, bf16[64,512]{0,1:T(8,128)(2,1)S(1)}, bf16[64,512]{0,1:T(8,128)(2,1)S(1)}, bf16[64,512]{1,0:T(8,128)(2,1)}, s32[]{:T(128)}, ...), branch_computations={%region_4.4_spmd, %region_5.7_spmd} | conditional | flops 483969664 | bytes 32420688 | solution.py:126
  266.7 1.0 copy.13
  271.3 1.1 convolution_convert_fusion
  273.5 1.2 fusion.8
  274.7 1.3 collective-permute-start.2
  276.8 7.1 %collective-permute-done.2 = bf16[64,1440]{1,0:T(8,128)(2,1)S(1)} collective-permute-done((bf16[64,1440]{1,0:T(8,128)(2,1)S(1)}, bf16[64,1440]{1,0:T(8,128)(2,1)S(1)}, u32[]{:S(2)}, u32[]{:S(2)}) %collective-permute-start.2) | collective-permute-done | bytes 184352 | tf_op jit(solution)/shard_map/while/body/eval_jaxpr/ppermute | solution.py:16
  287.3 9.2 %conditional.8 = (bf16[64,2048]{1,0:T(8,128)(2,1)S(1)}, bf16[64,512]{1,0:T(8,128)(2,1)}, bf16[64,512]{0,1:T(8,128)(2,1)}) conditional(s32[]{:T(128)} %convert_element_type.69, () %tuple.79, (bf16[64,1440]{1,0:T(8,128)(2,1)S(1)}, f32[1,1440]{1,0:T(1,128)S(1)}, bf16[1440,2048]{1,0:T(8,128)(2,1)}, f32[64,1,32]{2,0,1:T(8,128)S(1)}, ...), branch_computations={%region_1.1_spmd, %region_2.3_spmd} | conditional | flops 474183744 | bytes 12373788 | solution.py:124
  287.5 3.9 %fusion.26 = f32[64,2048]{1,0:T(8,128)S(1)} fusion(bf16[1440,2048]{1,0:T(8,128)(2,1)} %get-tuple-element.374, bf16[64,1440]{1,0:T(8,128)(2,1)S(1)} %get-tuple-element.372, f32[1440]{0:T(1024)S(1)} %reduce, f32[64]{0:T(128)S(1)} %add_rsqrt_fusion), kind=kOutput, calls=%fused_computation.44 | convolution fusion | flops 377856000 | bytes 6612864 | tf_op jit(solution)/shard_map/while/body/eval_jaxpr/cond/branch_1_fun/dot_general | solution.py:65
  294.9 1.6 copy.18
  296.5 2.3 collective-permute-start
  298.9 1.3 collective-permute-start.1
  302.0 1.5 bitcast_dynamic-update-slice_fusion.5
  303.5 8.0 %conditional.9 = (bf16[64,1440]{1,0:T(8,128)(2,1)S(1)}) conditional(s32[]{:T(128)} %convert_element_type.69, bf16[64,1440]{1,0:T(8,128)(2,1)S(1)} %bitcast_select_fusion.5, (bf16[64,1440]{1,0:T(8,128)(2,1)S(1)}, bf16[64,512]{0,1:T(8,128)(2,1)S(1)}, bf16[64,512]{0,1:T(8,128)(2,1)S(1)}, bf16[64,512]{1,0:T(8,128)(2,1)}, s32[]{:T(128)}, ...), branch_computations={%region_4.4_spmd, %region_5.7_spmd} | conditional | flops 483969664 | bytes 32420688 | solution.py:126
  308.0 1.1 convolution_convert_fusion
  310.2 1.2 fusion.8
  311.5 1.3 collective-permute-start.2
  313.5 7.1 %collective-permute-done.2 = bf16[64,1440]{1,0:T(8,128)(2,1)S(1)} collective-permute-done((bf16[64,1440]{1,0:T(8,128)(2,1)S(1)}, bf16[64,1440]{1,0:T(8,128)(2,1)S(1)}, u32[]{:S(2)}, u32[]{:S(2)}) %collective-permute-start.2) | collective-permute-done | bytes 184352 | tf_op jit(solution)/shard_map/while/body/eval_jaxpr/ppermute | solution.py:16
  324.1 9.2 %conditional.8 = (bf16[64,2048]{1,0:T(8,128)(2,1)S(1)}, bf16[64,512]{1,0:T(8,128)(2,1)}, bf16[64,512]{0,1:T(8,128)(2,1)}) conditional(s32[]{:T(128)} %convert_element_type.69, () %tuple.79, (bf16[64,1440]{1,0:T(8,128)(2,1)S(1)}, f32[1,1440]{1,0:T(1,128)S(1)}, bf16[1440,2048]{1,0:T(8,128)(2,1)}, f32[64,1,32]{2,0,1:T(8,128)S(1)}, ...), branch_computations={%region_1.1_spmd, %region_2.3_spmd} | conditional | flops 474183744 | bytes 12373788 | solution.py:124
  324.3 3.9 %fusion.26 = f32[64,2048]{1,0:T(8,128)S(1)} fusion(bf16[1440,2048]{1,0:T(8,128)(2,1)} %get-tuple-element.374, bf16[64,1440]{1,0:T(8,128)(2,1)S(1)} %get-tuple-element.372, f32[1440]{0:T(1024)S(1)} %reduce, f32[64]{0:T(128)S(1)} %add_rsqrt_fusion), kind=kOutput, calls=%fused_computation.44 | convolution fusion | flops 377856000 | bytes 6612864 | tf_op jit(solution)/shard_map/while/body/eval_jaxpr/cond/branch_1_fun/dot_general | solution.py:65
  331.7 1.6 copy.18
  333.3 2.3 collective-permute-start
  335.6 1.3 collective-permute-start.1
  338.7 1.5 bitcast_dynamic-update-slice_fusion.5
  340.2 8.0 %conditional.9 = (bf16[64,1440]{1,0:T(8,128)(2,1)S(1)}) conditional(s32[]{:T(128)} %convert_element_type.69, bf16[64,1440]{1,0:T(8,128)(2,1)S(1)} %bitcast_select_fusion.5, (bf16[64,1440]{1,0:T(8,128)(2,1)S(1)}, bf16[64,512]{0,1:T(8,128)(2,1)S(1)}, bf16[64,512]{0,1:T(8,128)(2,1)S(1)}, bf16[64,512]{1,0:T(8,128)(2,1)}, s32[]{:T(128)}, ...), branch_computations={%region_4.4_spmd, %region_5.7_spmd} | conditional | flops 483969664 | bytes 32420688 | solution.py:126
  344.8 1.1 convolution_convert_fusion
  347.0 1.2 fusion.8
  348.2 1.3 collective-permute-start.2
  350.3 6.8 %collective-permute-done.2 = bf16[64,1440]{1,0:T(8,128)(2,1)S(1)} collective-permute-done((bf16[64,1440]{1,0:T(8,128)(2,1)S(1)}, bf16[64,1440]{1,0:T(8,128)(2,1)S(1)}, u32[]{:S(2)}, u32[]{:S(2)}) %collective-permute-start.2) | collective-permute-done | bytes 184352 | tf_op jit(solution)/shard_map/while/body/eval_jaxpr/ppermute | solution.py:16
  (244 shorter events, 75.3 us)
Async XLA Ops:
  7.2 1.4 copy-start.1
  7.2 47.5 %all-gather.3.cloned.1.call-start = ((), (), s32[]{:S(2)}) async-start(), calls=%async_computation | async-start | bytes 7372800 | tf_op jit(solution)/shard_map/all_gather | solution.py:41
  7.9 2.8 copy-start.3
  7.9 94.7 %all-gather.5.cloned.1.call-start = ((), (), s32[]{:S(2)}) async-start(), calls=%async_computation.1 | async-start | bytes 7864320 | tf_op jit(solution)/shard_map/all_gather | solution.py:42
  10.2 94.1 %copy-start = (bf16[1,1440,512]{2,1,0:T(8,128)(2,1)S(1)}, bf16[1,1440,512]{2,1,0:T(8,128)(2,1)}, u32[]{:S(2)}) copy-start(bf16[1,1440,512]{2,1,0:T(8,128)(2,1)} %param.19) | copy-start | bytes 4423684
  10.2 94.1 %copy-start.2 = (f32[1,1440]{1,0:T(1,128)S(1)}, f32[1,1440]{1,0:T(1,128)}, u32[]{:S(2)}) copy-start(f32[1,1440]{1,0:T(1,128)} %param.17) | copy-start | bytes 17284
  10.2 94.1 %copy-start.4 = (s32[4]{0:T(128)S(1)}, s32[4]{0:T(128)}, u32[]{:S(2)}) copy-start(s32[4]{0:T(128)} %param.15) | copy-start | bytes 52
  10.2 94.1 %copy-start.5 = (s32[4]{0:T(128)S(1)}, s32[4]{0:T(128)}, u32[]{:S(2)}) copy-start(s32[4]{0:T(128)} %param.16) | copy-start | bytes 52
  109.1 6.8 %collective-permute-start = (bf16[64,512]{0,1:T(8,128)(2,1)}, bf16[64,512]{0,1:T(8,128)(2,1)S(1)}, u32[]{:S(2)}, u32[]{:S(2)}) collective-permute-start(bf16[64,512]{0,1:T(8,128)(2,1)} %get-tuple-element.696), channel_id=1, source_target_pairs={{0,2},{1,3},{4,6},{5,7},{8,10},{9,11},{12,14},{13,15},{16,18},{17,... | collective-permute-start | bytes 196616 | tf_op jit(solution)/shard_map/while/body/eval_jaxpr/ppermute | solution.py:16
  111.6 4.3 %collective-permute-start.1 = (bf16[64,512]{0,1:T(8,128)(2,1)}, bf16[64,512]{0,1:T(8,128)(2,1)S(1)}, u32[]{:S(2)}, u32[]{:S(2)}) collective-permute-start(bf16[64,512]{0,1:T(8,128)(2,1)} %get-tuple-element.696), channel_id=1, source_target_pairs={{0,1},{1,2},{2,3},{4,5},{5,6},{6,7},{8,9},{9,10},{10,11},{12,13},{... | collective-permute-start | bytes 196616 | tf_op jit(solution)/shard_map/while/body/eval_jaxpr/ppermute | solution.py:16
  116.0 9.3 %collective-permute-start.2 = (bf16[64,1440]{1,0:T(8,128)(2,1)S(1)}, bf16[64,1440]{1,0:T(8,128)(2,1)S(1)}, u32[]{:S(2)}, u32[]{:S(2)}) collective-permute-start(bf16[64,1440]{1,0:T(8,128)(2,1)S(1)} %get-tuple-element.771), channel_id=1, source_target_pairs={{0,4},{4,8},{8,12},{1,5},{5,9},{9,13},{2,6},{6,10},{10,14},{3,7},{... | collective-permute-start | bytes 552968 | tf_op jit(solution)/shard_map/while/body/eval_jaxpr/ppermute | solution.py:16
  130.1 6.8 %collective-permute-start = (bf16[64,512]{0,1:T(8,128)(2,1)}, bf16[64,512]{0,1:T(8,128)(2,1)S(1)}, u32[]{:S(2)}, u32[]{:S(2)}) collective-permute-start(bf16[64,512]{0,1:T(8,128)(2,1)} %get-tuple-element.696), channel_id=1, source_target_pairs={{0,2},{1,3},{4,6},{5,7},{8,10},{9,11},{12,14},{13,15},{16,18},{17,... | collective-permute-start | bytes 196616 | tf_op jit(solution)/shard_map/while/body/eval_jaxpr/ppermute | solution.py:16
  133.2 3.8 %collective-permute-start.1 = (bf16[64,512]{0,1:T(8,128)(2,1)}, bf16[64,512]{0,1:T(8,128)(2,1)S(1)}, u32[]{:S(2)}, u32[]{:S(2)}) collective-permute-start(bf16[64,512]{0,1:T(8,128)(2,1)} %get-tuple-element.696), channel_id=1, source_target_pairs={{0,1},{1,2},{2,3},{4,5},{5,6},{6,7},{8,9},{9,10},{10,11},{12,13},{... | collective-permute-start | bytes 196616 | tf_op jit(solution)/shard_map/while/body/eval_jaxpr/ppermute | solution.py:16
  137.0 9.2 %collective-permute-start.2 = (bf16[64,1440]{1,0:T(8,128)(2,1)S(1)}, bf16[64,1440]{1,0:T(8,128)(2,1)S(1)}, u32[]{:S(2)}, u32[]{:S(2)}) collective-permute-start(bf16[64,1440]{1,0:T(8,128)(2,1)S(1)} %get-tuple-element.771), channel_id=1, source_target_pairs={{0,4},{4,8},{8,12},{1,5},{5,9},{9,13},{2,6},{6,10},{10,14},{3,7},{... | collective-permute-start | bytes 552968 | tf_op jit(solution)/shard_map/while/body/eval_jaxpr/ppermute | solution.py:16
  151.0 6.8 %collective-permute-start = (bf16[64,512]{0,1:T(8,128)(2,1)}, bf16[64,512]{0,1:T(8,128)(2,1)S(1)}, u32[]{:S(2)}, u32[]{:S(2)}) collective-permute-start(bf16[64,512]{0,1:T(8,128)(2,1)} %get-tuple-element.696), channel_id=1, source_target_pairs={{0,2},{1,3},{4,6},{5,7},{8,10},{9,11},{12,14},{13,15},{16,18},{17,... | collective-permute-start | bytes 196616 | tf_op jit(solution)/shard_map/while/body/eval_jaxpr/ppermute | solution.py:16
  154.0 3.8 %collective-permute-start.1 = (bf16[64,512]{0,1:T(8,128)(2,1)}, bf16[64,512]{0,1:T(8,128)(2,1)S(1)}, u32[]{:S(2)}, u32[]{:S(2)}) collective-permute-start(bf16[64,512]{0,1:T(8,128)(2,1)} %get-tuple-element.696), channel_id=1, source_target_pairs={{0,1},{1,2},{2,3},{4,5},{5,6},{6,7},{8,9},{9,10},{10,11},{12,13},{... | collective-permute-start | bytes 196616 | tf_op jit(solution)/shard_map/while/body/eval_jaxpr/ppermute | solution.py:16
  157.8 52.5 %collective-permute-start.2 = (bf16[64,1440]{1,0:T(8,128)(2,1)S(1)}, bf16[64,1440]{1,0:T(8,128)(2,1)S(1)}, u32[]{:S(2)}, u32[]{:S(2)}) collective-permute-start(bf16[64,1440]{1,0:T(8,128)(2,1)S(1)} %get-tuple-element.771), channel_id=1, source_target_pairs={{0,4},{4,8},{8,12},{1,5},{5,9},{9,13},{2,6},{6,10},{10,14},{3,7},{... | collective-permute-start | bytes 552968 | tf_op jit(solution)/shard_map/while/body/eval_jaxpr/ppermute | solution.py:16
  223.0 6.9 %collective-permute-start = (bf16[64,512]{0,1:T(8,128)(2,1)}, bf16[64,512]{0,1:T(8,128)(2,1)S(1)}, u32[]{:S(2)}, u32[]{:S(2)}) collective-permute-start(bf16[64,512]{0,1:T(8,128)(2,1)} %get-tuple-element.696), channel_id=1, source_target_pairs={{0,2},{1,3},{4,6},{5,7},{8,10},{9,11},{12,14},{13,15},{16,18},{17,... | collective-permute-start | bytes 196616 | tf_op jit(solution)/shard_map/while/body/eval_jaxpr/ppermute | solution.py:16
  225.4 4.6 %collective-permute-start.1 = (bf16[64,512]{0,1:T(8,128)(2,1)}, bf16[64,512]{0,1:T(8,128)(2,1)S(1)}, u32[]{:S(2)}, u32[]{:S(2)}) collective-permute-start(bf16[64,512]{0,1:T(8,128)(2,1)} %get-tuple-element.696), channel_id=1, source_target_pairs={{0,1},{1,2},{2,3},{4,5},{5,6},{6,7},{8,9},{9,10},{10,11},{12,13},{... | collective-permute-start | bytes 196616 | tf_op jit(solution)/shard_map/while/body/eval_jaxpr/ppermute | solution.py:16
  233.7 2.2 slice-start
  234.5 2.2 slice-start.1
  238.0 9.1 %collective-permute-start.2 = (bf16[64,1440]{1,0:T(8,128)(2,1)S(1)}, bf16[64,1440]{1,0:T(8,128)(2,1)S(1)}, u32[]{:S(2)}, u32[]{:S(2)}) collective-permute-start(bf16[64,1440]{1,0:T(8,128)(2,1)S(1)} %get-tuple-element.771), channel_id=1, source_target_pairs={{0,4},{4,8},{8,12},{1,5},{5,9},{9,13},{2,6},{6,10},{10,14},{3,7},{... | collective-permute-start | bytes 552968 | tf_op jit(solution)/shard_map/while/body/eval_jaxpr/ppermute | solution.py:16
  259.8 6.9 %collective-permute-start = (bf16[64,512]{0,1:T(8,128)(2,1)}, bf16[64,512]{0,1:T(8,128)(2,1)S(1)}, u32[]{:S(2)}, u32[]{:S(2)}) collective-permute-start(bf16[64,512]{0,1:T(8,128)(2,1)} %get-tuple-element.696), channel_id=1, source_target_pairs={{0,2},{1,3},{4,6},{5,7},{8,10},{9,11},{12,14},{13,15},{16,18},{17,... | collective-permute-start | bytes 196616 | tf_op jit(solution)/shard_map/while/body/eval_jaxpr/ppermute | solution.py:16
  262.1 4.6 %collective-permute-start.1 = (bf16[64,512]{0,1:T(8,128)(2,1)}, bf16[64,512]{0,1:T(8,128)(2,1)S(1)}, u32[]{:S(2)}, u32[]{:S(2)}) collective-permute-start(bf16[64,512]{0,1:T(8,128)(2,1)} %get-tuple-element.696), channel_id=1, source_target_pairs={{0,1},{1,2},{2,3},{4,5},{5,6},{6,7},{8,9},{9,10},{10,11},{12,13},{... | collective-permute-start | bytes 196616 | tf_op jit(solution)/shard_map/while/body/eval_jaxpr/ppermute | solution.py:16
  270.4 2.2 slice-start
  271.3 2.2 slice-start.1
  274.7 9.1 %collective-permute-start.2 = (bf16[64,1440]{1,0:T(8,128)(2,1)S(1)}, bf16[64,1440]{1,0:T(8,128)(2,1)S(1)}, u32[]{:S(2)}, u32[]{:S(2)}) collective-permute-start(bf16[64,1440]{1,0:T(8,128)(2,1)S(1)} %get-tuple-element.771), channel_id=1, source_target_pairs={{0,4},{4,8},{8,12},{1,5},{5,9},{9,13},{2,6},{6,10},{10,14},{3,7},{... | collective-permute-start | bytes 552968 | tf_op jit(solution)/shard_map/while/body/eval_jaxpr/ppermute | solution.py:16
  296.5 6.9 %collective-permute-start = (bf16[64,512]{0,1:T(8,128)(2,1)}, bf16[64,512]{0,1:T(8,128)(2,1)S(1)}, u32[]{:S(2)}, u32[]{:S(2)}) collective-permute-start(bf16[64,512]{0,1:T(8,128)(2,1)} %get-tuple-element.696), channel_id=1, source_target_pairs={{0,2},{1,3},{4,6},{5,7},{8,10},{9,11},{12,14},{13,15},{16,18},{17,... | collective-permute-start | bytes 196616 | tf_op jit(solution)/shard_map/while/body/eval_jaxpr/ppermute | solution.py:16
  298.9 4.6 %collective-permute-start.1 = (bf16[64,512]{0,1:T(8,128)(2,1)}, bf16[64,512]{0,1:T(8,128)(2,1)S(1)}, u32[]{:S(2)}, u32[]{:S(2)}) collective-permute-start(bf16[64,512]{0,1:T(8,128)(2,1)} %get-tuple-element.696), channel_id=1, source_target_pairs={{0,1},{1,2},{2,3},{4,5},{5,6},{6,7},{8,9},{9,10},{10,11},{12,13},{... | collective-permute-start | bytes 196616 | tf_op jit(solution)/shard_map/while/body/eval_jaxpr/ppermute | solution.py:16
  307.1 2.2 slice-start
  308.0 2.2 slice-start.1
  311.5 9.1 %collective-permute-start.2 = (bf16[64,1440]{1,0:T(8,128)(2,1)S(1)}, bf16[64,1440]{1,0:T(8,128)(2,1)S(1)}, u32[]{:S(2)}, u32[]{:S(2)}) collective-permute-start(bf16[64,1440]{1,0:T(8,128)(2,1)S(1)} %get-tuple-element.771), channel_id=1, source_target_pairs={{0,4},{4,8},{8,12},{1,5},{5,9},{9,13},{2,6},{6,10},{10,14},{3,7},{... | collective-permute-start | bytes 552968 | tf_op jit(solution)/shard_map/while/body/eval_jaxpr/ppermute | solution.py:16
  333.3 6.9 %collective-permute-start = (bf16[64,512]{0,1:T(8,128)(2,1)}, bf16[64,512]{0,1:T(8,128)(2,1)S(1)}, u32[]{:S(2)}, u32[]{:S(2)}) collective-permute-start(bf16[64,512]{0,1:T(8,128)(2,1)} %get-tuple-element.696), channel_id=1, source_target_pairs={{0,2},{1,3},{4,6},{5,7},{8,10},{9,11},{12,14},{13,15},{16,18},{17,... | collective-permute-start | bytes 196616 | tf_op jit(solution)/shard_map/while/body/eval_jaxpr/ppermute | solution.py:16
  335.6 4.6 %collective-permute-start.1 = (bf16[64,512]{0,1:T(8,128)(2,1)}, bf16[64,512]{0,1:T(8,128)(2,1)S(1)}, u32[]{:S(2)}, u32[]{:S(2)}) collective-permute-start(bf16[64,512]{0,1:T(8,128)(2,1)} %get-tuple-element.696), channel_id=1, source_target_pairs={{0,1},{1,2},{2,3},{4,5},{5,6},{6,7},{8,9},{9,10},{10,11},{12,13},{... | collective-permute-start | bytes 196616 | tf_op jit(solution)/shard_map/while/body/eval_jaxpr/ppermute | solution.py:16
  343.9 2.2 slice-start
  344.8 2.2 slice-start.1
  348.2 8.8 %collective-permute-start.2 = (bf16[64,1440]{1,0:T(8,128)(2,1)S(1)}, bf16[64,1440]{1,0:T(8,128)(2,1)S(1)}, u32[]{:S(2)}, u32[]{:S(2)}) collective-permute-start(bf16[64,1440]{1,0:T(8,128)(2,1)S(1)} %get-tuple-element.771), channel_id=1, source_target_pairs={{0,4},{4,8},{8,12},{1,5},{5,9},{9,13},{2,6},{6,10},{10,14},{3,7},{... | collective-permute-start | bytes 552968 | tf_op jit(solution)/shard_map/while/body/eval_jaxpr/ppermute | solution.py:16
Sparse Core Ops, SparseCore 0:
  9.5 45.0 all-gather.2
  56.2 46.3 all-gather.4
where the time goes:
time: 366 us; the launch traced here: 364 us
  waiting for transfers between devices  185 us (51%)
  local copies, waits for them, and re-layouts  49.8 us (14%)
  starting transfers between devices  36.5 us (10%)
  other arithmetic  35.7 us (10%)
  matrix products  28.7 us (8%)
  loops' own time  14.3 us (4%)
  between operations  14.1 us (4%)
    ppermute x21, waiting for transfers between devices, from_behind(): return lax.ppermute(block, axis, route)  92.9 us
    all_gather x1, waiting for transfers between devices, per_device(): lax.all_gather(w_out, 'seq', axis=1, tiled=True)  47.9 us
    all_gather x1, waiting for transfers between devices, per_device(): lax.all_gather(w_query, 'seq', axis=2, tiled=True)  43.2 us
    ppermute x21, starting transfers between devices, from_behind(): return lax.ppermute(block, axis, route)  36.5 us
    dot_general x4, matrix products, project(): jnp.dot(normed, query_weight, preferred_element_type=jnp.float32)  15.5 us
    another operation x1, loops' own time, per_device(): final = lax.fori_loop(0, micro + sections - 1, turn, initial)  13.4 us
    dynamic_update_slice x7, other arithmetic, turn(): lax.dynamic_update_index_in_dim(cache_buffer, jnp.where(active, cache, pr...  7.9 us
    another operation x13, local copies, waits for them, and re-layouts  7.83 us
  transfers between devices with their start and end apart: 23, of which 9 were waited for; matrix products, arithmetic and copies ran while one was open for 8% of the time, Pallas kernels for 0%

commit v1 on v0

--- a/solution.py
+++ b/solution.py
@@ -8,6 +8,16 @@
 WIN = 128
 THETA = 150000.0
 EPSILON = 1e-05
+
+
+def drive_the_tokens(unit):
+    local_part = jnp.concatenate(
+        lax.all_to_all(
+            jnp.stack([unit] * lax.psum(1, "seq"), 0), "seq", split_axis=0, concat_axis=0
+        ),
+        1,
+    )
+    return local_part
 
 
 def from_behind(block, axis, distance):
@@ -39,7 +49,7 @@
     micro, rows, width = tokens.shape
     full_query, full_out = (
         lax.all_gather(w_query, "seq", axis=2, tiled=True),
-        lax.all_gather(w_out, "seq", axis=1, tiled=True),
+        drive_the_tokens(w_out),
     )
     query_weight = full_query[0]
     out_weight = full_out[0]

time: 366 us -> 378 us (1.033)
  local copies, waits for them, and re-layouts: 49.8 us -> 59.4 us
  starting transfers between devices: 36.5 us -> 43.1 us
  other arithmetic: 35.7 us -> 29.4 us
  waiting for transfers between devices: 185 us -> 189 us
    all_to_all x0 -> x1, waiting for transfers between devices: none -> 96.7 us  [drive_the_tokens(): lax.all_to_all(jnp.stack([unit] * lax.psum(1, 'seq'), 0), 'seq', split_ax...]
    all_gather x1 -> x0, waiting for transfers between devices: 47.9 us -> none  [per_device(): lax.all_gather(w_out, 'seq', axis=1, tiled=True)]
    all_gather x1, waiting for transfers between devices: 43.2 us -> 0.01 us  [per_device(): lax.all_gather(w_query, 'seq', axis=2, tiled=True)]
    unnamed x14, local copies, waits for them, and re-layouts: 2.72 us -> 9.61 us
    all_to_all x0 -> x1, starting transfers between devices: none -> 5.38 us  [drive_the_tokens(): lax.all_to_all(jnp.stack([unit] * lax.psum(1, 'seq'), 0), 'seq', split_ax...]
    reshape x4, local copies, waits for them, and re-layouts: 2.05 us -> 5.87 us  [attend(): grouped = queries.reshape(rows, kv_heads, group, HEAD_DIM)]
    another operation x13 -> x14, local copies, waits for them, and re-layouts: 7.83 us -> 7.66 us
  transfers between devices with their start and end apart: 23 -> 23, of which waited for: 9 -> 8; matrix products, arithmetic and copies ran while one was open for 8% -> 9% of each run, Pallas kernels for 0% -> 0%
where the time goes in v1:
time: 378 us; the launch traced here: 376 us
  waiting for transfers between devices  189 us (50%)
  local copies, waits for them, and re-layouts  59.4 us (16%)
  starting transfers between devices  43.1 us (11%)
  other arithmetic  29.4 us (8%)
  matrix products  28.7 us (8%)
  between operations  14.1 us (4%)
  loops' own time  13 us (3%)
    all_to_all x1, waiting for transfers between devices, drive_the_tokens(): lax.all_to_all(jnp.stack([unit] * lax.psum(1, 'seq'), 0), 'seq', split_ax...  96.7 us
    ppermute x21, waiting for transfers between devices, from_behind(): return lax.ppermute(block, axis, route)  91.2 us
    ppermute x21, starting transfers between devices, from_behind(): return lax.ppermute(block, axis, route)  37.7 us
    dot_general x4, matrix products, project(): jnp.dot(normed, query_weight, preferred_element_type=jnp.float32)  15.5 us
    another operation x1, loops' own time, per_device(): final = lax.fori_loop(0, micro + sections - 1, turn, initial)  12 us
    unnamed x14, local copies, waits for them, and re-layouts  9.61 us
  transfers between devices with their start and end apart: 23, of which 8 were waited for; matrix products, arithmetic and copies ran while one was open for 9% of the time, Pallas kernels for 0%

profile of v1, /device:TPU:28, one launch (start us, length us, event | category | flops | bytes accessed | tf_op | source)
XLA Modules:
  0.0 376.3 jit_solution(10556941721461217246)
XLA Ops:
  8.5 3.0 stack.2
  11.5 5.4 %all-to-all-start = ((bf16[4,1,512,1440]{2,3,1,0:T(8,128)(2,1)}), bf16[4,1,512,1440]{2,3,1,0:T(8,128)(2,1)}, u32[]{:S(2)}, u32[]{:S(2)}) async-start(bf16[4,1,512,1440]{2,3,1,0:T(8,128)(2,1)} %stack.2), calls=%async_computation | async-start | bytes 11796480 | tf_op jit(solution)/shard_map/all_to_all | solution.py:15
  18.3 96.7 %all-to-all-done = bf16[4,1,512,1440]{2,3,1,0:T(8,128)(2,1)} async-done(((bf16[4,1,512,1440]{2,3,1,0:T(8,128)(2,1)}), bf16[4,1,512,1440]{2,3,1,0:T(8,128)(2,1)}, u32[]{:S(2)}, u32[]{:S(2)}) %all-to-all-start) | async-done | bytes 5898272 | tf_op jit(solution)/shard_map/all_to_all | solution.py:15
  115.0 8.4 %copy.27 = bf16[4,1,512,1440]{3,2,0,1:T(8,128)(2,1)} copy(bf16[4,1,512,1440]{2,3,1,0:T(8,128)(2,1)} %all-to-all-done) | data formatting | bytes 11796480
  125.1 244.3 %while.20 = (s32[]{:T(128)}, bf16[64,1440]{1,0:T(8,128)(2,1)S(1)}, bf16[4,64,1440]{2,1,0:T(8,128)(2,1)}, bf16[4,64,512]{2,1,0:T(8,128)(2,1)}, s32[]{:T(128)}, /*...) while((s32[]{:T(128)}, bf16[64,1440]{1,0:T(8,128)(2,1)S(1)}, ...), condition=%wide.region_8.9_spmd.clone.clone, body=%wide.region_0.8_spmd.clone.clone.sunk | while | flops 958372544 | bytes 48405112 | solution.py:153
  128.4 1.4 conditional.8
  129.8 2.3 collective-permute-start
  132.1 1.5 collective-permute-start.1
  136.1 1.3 collective-permute-start.2
  138.2 7.3 %collective-permute-done.2 = bf16[64,1440]{1,0:T(8,128)(2,1)S(1)} collective-permute-done((bf16[64,1440]{1,0:T(8,128)(2,1)S(1)}, bf16[64,1440]{1,0:T(8,128)(2,1)S(1)}, u32[]{:S(2)}, u32[]{:S(2)}) %collective-permute-start.2) | collective-permute-done | bytes 184352 | tf_op jit(solution)/shard_map/while/body/eval_jaxpr/ppermute | solution.py:26
  148.7 1.4 conditional.8
  150.1 3.0 collective-permute-start
  153.1 1.3 collective-permute-start.1
  156.9 1.3 collective-permute-start.2
  159.0 7.2 %collective-permute-done.2 = bf16[64,1440]{1,0:T(8,128)(2,1)S(1)} collective-permute-done((bf16[64,1440]{1,0:T(8,128)(2,1)S(1)}, bf16[64,1440]{1,0:T(8,128)(2,1)S(1)}, u32[]{:S(2)}, u32[]{:S(2)}) %collective-permute-start.2) | collective-permute-done | bytes 184352 | tf_op jit(solution)/shard_map/while/body/eval_jaxpr/ppermute | solution.py:26
  169.4 1.4 conditional.8
  170.8 3.0 collective-permute-start
  173.8 1.3 collective-permute-start.1
  177.6 1.3 collective-permute-start.2
  179.6 47.2 %collective-permute-done.2 = bf16[64,1440]{1,0:T(8,128)(2,1)S(1)} collective-permute-done((bf16[64,1440]{1,0:T(8,128)(2,1)S(1)}, bf16[64,1440]{1,0:T(8,128)(2,1)S(1)}, u32[]{:S(2)}, u32[]{:S(2)}) %collective-permute-start.2) | collective-permute-done | bytes 184352 | tf_op jit(solution)/shard_map/while/body/eval_jaxpr/ppermute | solution.py:26
  230.1 8.5 %conditional.8 = (bf16[64,2048]{1,0:T(8,128)(2,1)}, bf16[64,512]{1,0:T(8,128)(2,1)S(1)}, bf16[64,512]{0,1:T(8,128)(2,1)}) conditional(s32[]{:T(128)} %convert_element_type.69, () %tuple.82, (bf16[64,1440]{1,0:T(8,128)(2,1)S(1)}, f32[1,1440]{1,0:T(1,128)S(1)}, bf16[1440,2048]{1,0:T(8,128)(2,1)}, f32[64,1,32]{2,0,1:T(8,128)S(1)}, ...), branch_computations={%region_1.1_spmd, %region_2.3_spmd} | conditional | flops 474183744 | bytes 12898132 | solution.py:134
  232.3 3.9 %fusion.26 = f32[64,2048]{1,0:T(8,128)S(1)} fusion(bf16[1440,2048]{1,0:T(8,128)(2,1)} %get-tuple-element.374, bf16[64,1440]{1,0:T(8,128)(2,1)S(1)} %get-tuple-element.372, f32[1440]{0:T(1024)S(1)} %reduce, f32[64]{0:T(128)S(1)} %add_rsqrt_fusion), kind=kOutput, calls=%fused_computation.44 | convolution fusion | flops 377856000 | bytes 6612864 | tf_op jit(solution)/shard_map/while/body/eval_jaxpr/cond/branch_1_fun/dot_general | solution.py:75
  237.4 1.2 convert_element_type.37
  238.6 2.7 collective-permute-start
  241.3 1.3 collective-permute-start.1
  245.1 8.0 %conditional.9 = (bf16[64,1440]{1,0:T(8,128)(2,1)S(1)}) conditional(s32[]{:T(128)} %convert_element_type.69, bf16[64,1440]{1,0:T(8,128)(2,1)S(1)} %bitcast_select_fusion.5, (bf16[64,1440]{1,0:T(8,128)(2,1)S(1)}, bf16[64,512]{0,1:T(8,128)(2,1)S(1)}, bf16[64,512]{0,1:T(8,128)(2,1)S(1)}, bf16[64,512]{1,0:T(8,128)(2,1)S(1)}, s32[]{:T(128)}, ...), branch_computations={%region_4.4_spmd, %region_5.7_spmd} | conditional | flops 483969664 | bytes 32420688 | solution.py:136
  246.7 1.5 reshape.145
  249.7 1.1 convolution_convert_fusion
  251.9 1.2 fusion.8
  253.1 1.3 collective-permute-start.2
  255.1 7.4 %collective-permute-done.2 = bf16[64,1440]{1,0:T(8,128)(2,1)S(1)} collective-permute-done((bf16[64,1440]{1,0:T(8,128)(2,1)S(1)}, bf16[64,1440]{1,0:T(8,128)(2,1)S(1)}, u32[]{:S(2)}, u32[]{:S(2)}) %collective-permute-start.2) | collective-permute-done | bytes 184352 | tf_op jit(solution)/shard_map/while/body/eval_jaxpr/ppermute | solution.py:26
  265.8 8.4 %conditional.8 = (bf16[64,2048]{1,0:T(8,128)(2,1)}, bf16[64,512]{1,0:T(8,128)(2,1)S(1)}, bf16[64,512]{0,1:T(8,128)(2,1)}) conditional(s32[]{:T(128)} %convert_element_type.69, () %tuple.82, (bf16[64,1440]{1,0:T(8,128)(2,1)S(1)}, f32[1,1440]{1,0:T(1,128)S(1)}, bf16[1440,2048]{1,0:T(8,128)(2,1)}, f32[64,1,32]{2,0,1:T(8,128)S(1)}, ...), branch_computations={%region_1.1_spmd, %region_2.3_spmd} | conditional | flops 474183744 | bytes 12898132 | solution.py:134
  268.0 3.9 %fusion.26 = f32[64,2048]{1,0:T(8,128)S(1)} fusion(bf16[1440,2048]{1,0:T(8,128)(2,1)} %get-tuple-element.374, bf16[64,1440]{1,0:T(8,128)(2,1)S(1)} %get-tuple-element.372, f32[1440]{0:T(1024)S(1)} %reduce, f32[64]{0:T(128)S(1)} %add_rsqrt_fusion), kind=kOutput, calls=%fused_computation.44 | convolution fusion | flops 377856000 | bytes 6612864 | tf_op jit(solution)/shard_map/while/body/eval_jaxpr/cond/branch_1_fun/dot_general | solution.py:75
  273.1 1.2 convert_element_type.37
  274.3 2.8 collective-permute-start
  277.0 1.3 collective-permute-start.1
  280.8 8.0 %conditional.9 = (bf16[64,1440]{1,0:T(8,128)(2,1)S(1)}) conditional(s32[]{:T(128)} %convert_element_type.69, bf16[64,1440]{1,0:T(8,128)(2,1)S(1)} %bitcast_select_fusion.5, (bf16[64,1440]{1,0:T(8,128)(2,1)S(1)}, bf16[64,512]{0,1:T(8,128)(2,1)S(1)}, bf16[64,512]{0,1:T(8,128)(2,1)S(1)}, bf16[64,512]{1,0:T(8,128)(2,1)S(1)}, s32[]{:T(128)}, ...), branch_computations={%region_4.4_spmd, %region_5.7_spmd} | conditional | flops 483969664 | bytes 32420688 | solution.py:136
  282.4 1.5 reshape.145
  285.4 1.1 convolution_convert_fusion
  287.6 1.2 fusion.8
  288.8 1.3 collective-permute-start.2
  290.9 7.4 %collective-permute-done.2 = bf16[64,1440]{1,0:T(8,128)(2,1)S(1)} collective-permute-done((bf16[64,1440]{1,0:T(8,128)(2,1)S(1)}, bf16[64,1440]{1,0:T(8,128)(2,1)S(1)}, u32[]{:S(2)}, u32[]{:S(2)}) %collective-permute-start.2) | collective-permute-done | bytes 184352 | tf_op jit(solution)/shard_map/while/body/eval_jaxpr/ppermute | solution.py:26
  301.6 8.4 %conditional.8 = (bf16[64,2048]{1,0:T(8,128)(2,1)}, bf16[64,512]{1,0:T(8,128)(2,1)S(1)}, bf16[64,512]{0,1:T(8,128)(2,1)}) conditional(s32[]{:T(128)} %convert_element_type.69, () %tuple.82, (bf16[64,1440]{1,0:T(8,128)(2,1)S(1)}, f32[1,1440]{1,0:T(1,128)S(1)}, bf16[1440,2048]{1,0:T(8,128)(2,1)}, f32[64,1,32]{2,0,1:T(8,128)S(1)}, ...), branch_computations={%region_1.1_spmd, %region_2.3_spmd} | conditional | flops 474183744 | bytes 12898132 | solution.py:134
  303.7 3.9 %fusion.26 = f32[64,2048]{1,0:T(8,128)S(1)} fusion(bf16[1440,2048]{1,0:T(8,128)(2,1)} %get-tuple-element.374, bf16[64,1440]{1,0:T(8,128)(2,1)S(1)} %get-tuple-element.372, f32[1440]{0:T(1024)S(1)} %reduce, f32[64]{0:T(128)S(1)} %add_rsqrt_fusion), kind=kOutput, calls=%fused_computation.44 | convolution fusion | flops 377856000 | bytes 6612864 | tf_op jit(solution)/shard_map/while/body/eval_jaxpr/cond/branch_1_fun/dot_general | solution.py:75
  308.8 1.2 convert_element_type.37
  310.0 2.8 collective-permute-start
  312.8 1.3 collective-permute-start.1
  316.5 8.0 %conditional.9 = (bf16[64,1440]{1,0:T(8,128)(2,1)S(1)}) conditional(s32[]{:T(128)} %convert_element_type.69, bf16[64,1440]{1,0:T(8,128)(2,1)S(1)} %bitcast_select_fusion.5, (bf16[64,1440]{1,0:T(8,128)(2,1)S(1)}, bf16[64,512]{0,1:T(8,128)(2,1)S(1)}, bf16[64,512]{0,1:T(8,128)(2,1)S(1)}, bf16[64,512]{1,0:T(8,128)(2,1)S(1)}, s32[]{:T(128)}, ...), branch_computations={%region_4.4_spmd, %region_5.7_spmd} | conditional | flops 483969664 | bytes 32420688 | solution.py:136
  318.1 1.5 reshape.145
  321.1 1.1 convolution_convert_fusion
  323.3 1.2 fusion.8
  324.6 1.3 collective-permute-start.2
  326.6 7.4 %collective-permute-done.2 = bf16[64,1440]{1,0:T(8,128)(2,1)S(1)} collective-permute-done((bf16[64,1440]{1,0:T(8,128)(2,1)S(1)}, bf16[64,1440]{1,0:T(8,128)(2,1)S(1)}, u32[]{:S(2)}, u32[]{:S(2)}) %collective-permute-start.2) | collective-permute-done | bytes 184352 | tf_op jit(solution)/shard_map/while/body/eval_jaxpr/ppermute | solution.py:26
  337.3 8.4 %conditional.8 = (bf16[64,2048]{1,0:T(8,128)(2,1)}, bf16[64,512]{1,0:T(8,128)(2,1)S(1)}, bf16[64,512]{0,1:T(8,128)(2,1)}) conditional(s32[]{:T(128)} %convert_element_type.69, () %tuple.82, (bf16[64,1440]{1,0:T(8,128)(2,1)S(1)}, f32[1,1440]{1,0:T(1,128)S(1)}, bf16[1440,2048]{1,0:T(8,128)(2,1)}, f32[64,1,32]{2,0,1:T(8,128)S(1)}, ...), branch_computations={%region_1.1_spmd, %region_2.3_spmd} | conditional | flops 474183744 | bytes 12898132 | solution.py:134
  339.5 3.9 %fusion.26 = f32[64,2048]{1,0:T(8,128)S(1)} fusion(bf16[1440,2048]{1,0:T(8,128)(2,1)} %get-tuple-element.374, bf16[64,1440]{1,0:T(8,128)(2,1)S(1)} %get-tuple-element.372, f32[1440]{0:T(1024)S(1)} %reduce, f32[64]{0:T(128)S(1)} %add_rsqrt_fusion), kind=kOutput, calls=%fused_computation.44 | convolution fusion | flops 377856000 | bytes 6612864 | tf_op jit(solution)/shard_map/while/body/eval_jaxpr/cond/branch_1_fun/dot_general | solution.py:75
  344.5 1.2 convert_element_type.37
  345.7 2.8 collective-permute-start
  348.5 1.3 collective-permute-start.1
  352.3 8.0 %conditional.9 = (bf16[64,1440]{1,0:T(8,128)(2,1)S(1)}) conditional(s32[]{:T(128)} %convert_element_type.69, bf16[64,1440]{1,0:T(8,128)(2,1)S(1)} %bitcast_select_fusion.5, (bf16[64,1440]{1,0:T(8,128)(2,1)S(1)}, bf16[64,512]{0,1:T(8,128)(2,1)S(1)}, bf16[64,512]{0,1:T(8,128)(2,1)S(1)}, bf16[64,512]{1,0:T(8,128)(2,1)S(1)}, s32[]{:T(128)}, ...), branch_computations={%region_4.4_spmd, %region_5.7_spmd} | conditional | flops 483969664 | bytes 32420688 | solution.py:136
  353.8 1.5 reshape.145
  356.8 1.1 convolution_convert_fusion
  359.0 1.2 fusion.8
  360.3 1.3 collective-permute-start.2
  362.3 7.2 %collective-permute-done.2 = bf16[64,1440]{1,0:T(8,128)(2,1)S(1)} collective-permute-done((bf16[64,1440]{1,0:T(8,128)(2,1)S(1)}, bf16[64,1440]{1,0:T(8,128)(2,1)S(1)}, u32[]{:S(2)}, u32[]{:S(2)}) %collective-permute-start.2) | collective-permute-done | bytes 184352 | tf_op jit(solution)/shard_map/while/body/eval_jaxpr/ppermute | solution.py:26
  (260 shorter events, 71.5 us)
Async XLA Ops:
  7.2 1.4 copy-start.3
  7.2 116.2 %all-gather.2.cloned.1.call-start = ((), (), s32[]{:S(2)}) async-start(), calls=%async_computation.1 | async-start | bytes 7372800 | tf_op jit(solution)/shard_map/all_gather | solution.py:51
  11.5 5.9 %copy-start.5 = (f32[1,32]{1,0:T(1,128)S(1)}, f32[1,32]{1,0:T(1,128)}, u32[]{:S(2)}) copy-start(f32[1,32]{1,0:T(1,128)} %param.21) | copy-start | bytes 388
  11.5 103.4 %all-to-all-start = ((bf16[4,1,512,1440]{2,3,1,0:T(8,128)(2,1)}), bf16[4,1,512,1440]{2,3,1,0:T(8,128)(2,1)}, u32[]{:S(2)}, u32[]{:S(2)}) async-start(bf16[4,1,512,1440]{2,3,1,0:T(8,128)(2,1)} %stack.2), calls=%async_computation | async-start | bytes 11796480 | tf_op jit(solution)/shard_map/all_to_all | solution.py:15
  18.2 106.9 %copy-start = (bf16[1,1440,512]{2,1,0:T(8,128)(2,1)S(1)}, bf16[1,1440,512]{2,1,0:T(8,128)(2,1)}, u32[]{:S(2)}) copy-start(bf16[1,1440,512]{2,1,0:T(8,128)(2,1)} %param.19) | copy-start | bytes 4423684
  18.2 106.9 %copy-start.4 = (f32[1,1440]{1,0:T(1,128)S(1)}, f32[1,1440]{1,0:T(1,128)}, u32[]{:S(2)}) copy-start(f32[1,1440]{1,0:T(1,128)} %param.17) | copy-start | bytes 17284
  18.2 106.9 %copy-start.6 = (s32[4]{0:T(128)S(1)}, s32[4]{0:T(128)}, u32[]{:S(2)}) copy-start(s32[4]{0:T(128)} %param.15) | copy-start | bytes 52
  18.3 106.9 %copy-start.7 = (s32[4]{0:T(128)S(1)}, s32[4]{0:T(128)}, u32[]{:S(2)}) copy-start(s32[4]{0:T(128)} %param.16) | copy-start | bytes 52
  129.8 6.3 %collective-permute-start = (bf16[64,512]{0,1:T(8,128)(2,1)}, bf16[64,512]{0,1:T(8,128)(2,1)S(1)}, u32[]{:S(2)}, u32[]{:S(2)}) collective-permute-start(bf16[64,512]{0,1:T(8,128)(2,1)} %get-tuple-element.736), channel_id=1, source_target_pairs={{0,2},{1,3},{4,6},{5,7},{8,10},{9,11},{12,14},{13,15},{16,18},{17,... | collective-permute-start | bytes 196616 | tf_op jit(solution)/shard_map/while/body/eval_jaxpr/ppermute | solution.py:26
  132.1 4.0 %collective-permute-start.1 = (bf16[64,512]{0,1:T(8,128)(2,1)}, bf16[64,512]{0,1:T(8,128)(2,1)S(1)}, u32[]{:S(2)}, u32[]{:S(2)}) collective-permute-start(bf16[64,512]{0,1:T(8,128)(2,1)} %get-tuple-element.736), channel_id=1, source_target_pairs={{0,1},{1,2},{2,3},{4,5},{5,6},{6,7},{8,9},{9,10},{10,11},{12,13},{... | collective-permute-start | bytes 196616 | tf_op jit(solution)/shard_map/while/body/eval_jaxpr/ppermute | solution.py:26
  136.1 9.3 %collective-permute-start.2 = (bf16[64,1440]{1,0:T(8,128)(2,1)S(1)}, bf16[64,1440]{1,0:T(8,128)(2,1)S(1)}, u32[]{:S(2)}, u32[]{:S(2)}) collective-permute-start(bf16[64,1440]{1,0:T(8,128)(2,1)S(1)} %get-tuple-element.811), channel_id=1, source_target_pairs={{0,4},{4,8},{8,12},{1,5},{5,9},{9,13},{2,6},{6,10},{10,14},{3,7},{... | collective-permute-start | bytes 552968 | tf_op jit(solution)/shard_map/while/body/eval_jaxpr/ppermute | solution.py:26
  150.1 6.8 %collective-permute-start = (bf16[64,512]{0,1:T(8,128)(2,1)}, bf16[64,512]{0,1:T(8,128)(2,1)S(1)}, u32[]{:S(2)}, u32[]{:S(2)}) collective-permute-start(bf16[64,512]{0,1:T(8,128)(2,1)} %get-tuple-element.736), channel_id=1, source_target_pairs={{0,2},{1,3},{4,6},{5,7},{8,10},{9,11},{12,14},{13,15},{16,18},{17,... | collective-permute-start | bytes 196616 | tf_op jit(solution)/shard_map/while/body/eval_jaxpr/ppermute | solution.py:26
  153.1 3.8 collective-permute-start.1
  156.9 9.2 %collective-permute-start.2 = (bf16[64,1440]{1,0:T(8,128)(2,1)S(1)}, bf16[64,1440]{1,0:T(8,128)(2,1)S(1)}, u32[]{:S(2)}, u32[]{:S(2)}) collective-permute-start(bf16[64,1440]{1,0:T(8,128)(2,1)S(1)} %get-tuple-element.811), channel_id=1, source_target_pairs={{0,4},{4,8},{8,12},{1,5},{5,9},{9,13},{2,6},{6,10},{10,14},{3,7},{... | collective-permute-start | bytes 552968 | tf_op jit(solution)/shard_map/while/body/eval_jaxpr/ppermute | solution.py:26
  170.8 6.8 %collective-permute-start = (bf16[64,512]{0,1:T(8,128)(2,1)}, bf16[64,512]{0,1:T(8,128)(2,1)S(1)}, u32[]{:S(2)}, u32[]{:S(2)}) collective-permute-start(bf16[64,512]{0,1:T(8,128)(2,1)} %get-tuple-element.736), channel_id=1, source_target_pairs={{0,2},{1,3},{4,6},{5,7},{8,10},{9,11},{12,14},{13,15},{16,18},{17,... | collective-permute-start | bytes 196616 | tf_op jit(solution)/shard_map/while/body/eval_jaxpr/ppermute | solution.py:26
  173.8 3.8 collective-permute-start.1
  177.6 49.3 %collective-permute-start.2 = (bf16[64,1440]{1,0:T(8,128)(2,1)S(1)}, bf16[64,1440]{1,0:T(8,128)(2,1)S(1)}, u32[]{:S(2)}, u32[]{:S(2)}) collective-permute-start(bf16[64,1440]{1,0:T(8,128)(2,1)S(1)} %get-tuple-element.811), channel_id=1, source_target_pairs={{0,4},{4,8},{8,12},{1,5},{5,9},{9,13},{2,6},{6,10},{10,14},{3,7},{... | collective-permute-start | bytes 552968 | tf_op jit(solution)/shard_map/while/body/eval_jaxpr/ppermute | solution.py:26
  231.5 4.6 %copy-start.1 = (bf16[64,512]{1,0:T(8,128)(2,1)}, bf16[64,512]{1,0:T(8,128)(2,1)S(1)}, u32[]{:S(2)}) copy-start(bf16[64,512]{1,0:T(8,128)(2,1)S(1)} %pad_maximum_fusion.3) | copy-start | bytes 196612 | tf_op jit(solution)/shard_map/while/body/eval_jaxpr/cond
  236.6 2.0 copy-start.2
  238.6 6.5 %collective-permute-start = (bf16[64,512]{0,1:T(8,128)(2,1)}, bf16[64,512]{0,1:T(8,128)(2,1)S(1)}, u32[]{:S(2)}, u32[]{:S(2)}) collective-permute-start(bf16[64,512]{0,1:T(8,128)(2,1)} %get-tuple-element.736), channel_id=1, source_target_pairs={{0,2},{1,3},{4,6},{5,7},{8,10},{9,11},{12,14},{13,15},{16,18},{17,... | collective-permute-start | bytes 196616 | tf_op jit(solution)/shard_map/while/body/eval_jaxpr/ppermute | solution.py:26
  241.3 3.8 collective-permute-start.1
  248.8 2.2 slice-start
  249.6 2.2 slice-start.1
  253.1 9.5 %collective-permute-start.2 = (bf16[64,1440]{1,0:T(8,128)(2,1)S(1)}, bf16[64,1440]{1,0:T(8,128)(2,1)S(1)}, u32[]{:S(2)}, u32[]{:S(2)}) collective-permute-start(bf16[64,1440]{1,0:T(8,128)(2,1)S(1)} %get-tuple-element.811), channel_id=1, source_target_pairs={{0,4},{4,8},{8,12},{1,5},{5,9},{9,13},{2,6},{6,10},{10,14},{3,7},{... | collective-permute-start | bytes 552968 | tf_op jit(solution)/shard_map/while/body/eval_jaxpr/ppermute | solution.py:26
  267.2 4.6 %copy-start.1 = (bf16[64,512]{1,0:T(8,128)(2,1)}, bf16[64,512]{1,0:T(8,128)(2,1)S(1)}, u32[]{:S(2)}) copy-start(bf16[64,512]{1,0:T(8,128)(2,1)S(1)} %pad_maximum_fusion.3) | copy-start | bytes 196612 | tf_op jit(solution)/shard_map/while/body/eval_jaxpr/cond
  272.3 2.0 copy-start.2
  274.3 6.5 %collective-permute-start = (bf16[64,512]{0,1:T(8,128)(2,1)}, bf16[64,512]{0,1:T(8,128)(2,1)S(1)}, u32[]{:S(2)}, u32[]{:S(2)}) collective-permute-start(bf16[64,512]{0,1:T(8,128)(2,1)} %get-tuple-element.736), channel_id=1, source_target_pairs={{0,2},{1,3},{4,6},{5,7},{8,10},{9,11},{12,14},{13,15},{16,18},{17,... | collective-permute-start | bytes 196616 | tf_op jit(solution)/shard_map/while/body/eval_jaxpr/ppermute | solution.py:26
  277.0 3.8 collective-permute-start.1
  284.5 2.2 slice-start
  285.4 2.2 slice-start.1
  288.8 9.5 %collective-permute-start.2 = (bf16[64,1440]{1,0:T(8,128)(2,1)S(1)}, bf16[64,1440]{1,0:T(8,128)(2,1)S(1)}, u32[]{:S(2)}, u32[]{:S(2)}) collective-permute-start(bf16[64,1440]{1,0:T(8,128)(2,1)S(1)} %get-tuple-element.811), channel_id=1, source_target_pairs={{0,4},{4,8},{8,12},{1,5},{5,9},{9,13},{2,6},{6,10},{10,14},{3,7},{... | collective-permute-start | bytes 552968 | tf_op jit(solution)/shard_map/while/body/eval_jaxpr/ppermute | solution.py:26
  303.0 4.6 %copy-start.1 = (bf16[64,512]{1,0:T(8,128)(2,1)}, bf16[64,512]{1,0:T(8,128)(2,1)S(1)}, u32[]{:S(2)}) copy-start(bf16[64,512]{1,0:T(8,128)(2,1)S(1)} %pad_maximum_fusion.3) | copy-start | bytes 196612 | tf_op jit(solution)/shard_map/while/body/eval_jaxpr/cond
  308.0 2.0 copy-start.2
  310.0 6.5 %collective-permute-start = (bf16[64,512]{0,1:T(8,128)(2,1)}, bf16[64,512]{0,1:T(8,128)(2,1)S(1)}, u32[]{:S(2)}, u32[]{:S(2)}) collective-permute-start(bf16[64,512]{0,1:T(8,128)(2,1)} %get-tuple-element.736), channel_id=1, source_target_pairs={{0,2},{1,3},{4,6},{5,7},{8,10},{9,11},{12,14},{13,15},{16,18},{17,... | collective-permute-start | bytes 196616 | tf_op jit(solution)/shard_map/while/body/eval_jaxpr/ppermute | solution.py:26
  312.8 3.8 collective-permute-start.1
  320.2 2.2 slice-start
  321.1 2.2 slice-start.1
  324.6 9.5 %collective-permute-start.2 = (bf16[64,1440]{1,0:T(8,128)(2,1)S(1)}, bf16[64,1440]{1,0:T(8,128)(2,1)S(1)}, u32[]{:S(2)}, u32[]{:S(2)}) collective-permute-start(bf16[64,1440]{1,0:T(8,128)(2,1)S(1)} %get-tuple-element.811), channel_id=1, source_target_pairs={{0,4},{4,8},{8,12},{1,5},{5,9},{9,13},{2,6},{6,10},{10,14},{3,7},{... | collective-permute-start | bytes 552968 | tf_op jit(solution)/shard_map/while/body/eval_jaxpr/ppermute | solution.py:26
  338.7 4.6 %copy-start.1 = (bf16[64,512]{1,0:T(8,128)(2,1)}, bf16[64,512]{1,0:T(8,128)(2,1)S(1)}, u32[]{:S(2)}) copy-start(bf16[64,512]{1,0:T(8,128)(2,1)S(1)} %pad_maximum_fusion.3) | copy-start | bytes 196612 | tf_op jit(solution)/shard_map/while/body/eval_jaxpr/cond
  343.8 2.0 copy-start.2
  345.7 6.5 %collective-permute-start = (bf16[64,512]{0,1:T(8,128)(2,1)}, bf16[64,512]{0,1:T(8,128)(2,1)S(1)}, u32[]{:S(2)}, u32[]{:S(2)}) collective-permute-start(bf16[64,512]{0,1:T(8,128)(2,1)} %get-tuple-element.736), channel_id=1, source_target_pairs={{0,2},{1,3},{4,6},{5,7},{8,10},{9,11},{12,14},{13,15},{16,18},{17,... | collective-permute-start | bytes 196616 | tf_op jit(solution)/shard_map/while/body/eval_jaxpr/ppermute | solution.py:26
  348.5 3.8 collective-permute-start.1
  355.9 2.2 slice-start
  356.8 2.2 slice-start.1
  360.3 9.2 %collective-permute-start.2 = (bf16[64,1440]{1,0:T(8,128)(2,1)S(1)}, bf16[64,1440]{1,0:T(8,128)(2,1)S(1)}, u32[]{:S(2)}, u32[]{:S(2)}) collective-permute-start(bf16[64,1440]{1,0:T(8,128)(2,1)S(1)} %get-tuple-element.811), channel_id=1, source_target_pairs={{0,4},{4,8},{8,12},{1,5},{5,9},{9,13},{2,6},{6,10},{10,14},{3,7},{... | collective-permute-start | bytes 552968 | tf_op jit(solution)/shard_map/while/body/eval_jaxpr/ppermute | solution.py:26
Sparse Core Ops, SparseCore 0:
  9.5 76.7 all-gather.1
